TPU v7x, 32 devices: a whole 2x2x4 slice. The times are simulated.
32 devices in a mesh: gy: 4 (over x, core), gx: 8 (over z, y).
Axes of the slice: x: 2, y: 2, z: 4, core: 2. Of those that a mesh axis runs over, the one named last changes fastest.
Arguments:
- first_factor: bfloat16 [4096, 2048], P('gy', 'gx'), may hold values from -6 to 6
- second_factor: bfloat16 [2048, 8192], P('gy', 'gx'), may hold values from -0.125 to 0.125
- result_in: float32 [4096, 8192], P('gy', 'gx'), may hold values from -6 to 6
- pivot_scale: float32 [2048], replicated, may hold values from 0.25 to 1.75
Outputs:
- corrected: float32 [4096, 8192], P('gy', 'gx')
All inputs are finite; a program needn't handle non-finite values.
Results may differ from a plain program's by a relative error of at most 0.002.
Values may be sent and summed in bfloat16 or wider, within the bound.
A program may use at most 128 MiB of HBM per device.

v0:
```python
import jax
import jax.numpy as jnp
from jax import lax
from jax.sharding import PartitionSpec as P


def join_panel(left_panel, right_panel):
    return jnp.dot(left_panel, right_panel, preferred_element_type=jnp.float32)


def shards(first_factor, second_factor, result_in, pivot_scale):
    share = first_factor.shape[1]
    part_scale = lax.dynamic_slice_in_dim(pivot_scale, lax.axis_index("gx") * share, share)
    scaled_left = (first_factor.astype(jnp.float32) * part_scale).astype(jnp.bfloat16)
    left_line = lax.all_gather(scaled_left, "gx", axis=1, tiled=True)
    total = join_panel(left_line, lax.all_gather(second_factor, "gy", axis=0, tiled=True))
    corrected = result_in - total
    row_power = lax.psum(jnp.sum(corrected * corrected, axis=1), "gx")
    corrected = (
        corrected
        * lax.rsqrt(row_power / (corrected.shape[1] * lax.axis_size("gx")) + 1e-06)[:, None]
    )
    return corrected


def solution(mesh):
    return jax.shard_map(
        shards,
        mesh=mesh,
        in_specs=(P("gy", "gx"), P("gy", "gx"), P("gy", "gx"), P()),
        out_specs=P("gy", "gx"),
        check_vma=False,
    )
```

profile of v0, /device:TPU:0, one launch (start us, length us, event | category | flops | bytes accessed | tf_op | source)
XLA Modules:
  0.0 169.9 jit_solution(15891152812098854044)
XLA Ops:
  6.5 0.0 all-gather.5.cloned.1.call-start
  6.5 0.7 all-gather.5.cloned.1.call-update
  7.3 0.0 all-gather.3.cloned.1.call-start
  7.3 0.8 dynamic_slice.3
  8.1 2.0 %multiply_convert_fusion = bf16[1024,256]{1,0:T(8,128)(2,1)} fusion(bf16[1024,256]{1,0:T(8,128)(2,1)} %param.4, f32[256]{0:T(256)S(1)} %dynamic_slice.3), kind=kLoop, calls=%fused_computation.3 | loop fusion | flops 786432 | bytes 1049600 | tf_op jit(solution)/shard_map/convert_element_type | solution.py:14
  10.1 0.0 all-gather.3.cloned.1.call-update
  10.1 5.3 %copy.5 = f32[1024,1024]{0,1:T(8,128)} copy(f32[1024,1024]{1,0:T(8,128)} %param.6) | data formatting | bytes 8388608 | tf_op args[2]
  15.4 30.7 %all-gather.5.cloned.1.call-done = bf16[2048,1024]{1,0:T(8,128)(2,1)} async-done(((bf16[512,1024]{1,0:T(8,128)(2,1)}), bf16[2048,1024]{1,0:T(8,128)(2,1)}) %all-gather.5.cloned.1.call-update) | async-done | bytes 4194320 | tf_op jit(solution)/shard_map/all_gather | solution.py:16
  46.1 76.7 %all-gather.3.cloned.1.call-done = bf16[1024,2048]{1,0:T(8,128)(2,1)} async-done(((bf16[1024,256]{1,0:T(8,128)(2,1)}), bf16[1024,2048]{1,0:T(8,128)(2,1)}) %all-gather.3.cloned.1.call-update) | async-done | bytes 4194320 | tf_op jit(solution)/shard_map/all_gather | solution.py:15
  122.8 11.3 %multiply_reduce_fusion = (f32[1024]{0:T(1024)S(1)}, f32[1024,1024]{0,1:T(8,128)}) fusion(f32[1024,1024]{0,1:T(8,128)} %copy.5, bf16[1024,2048]{1,0:T(8,128)(2,1)} %all-gather.3.cloned.1.call-done, bf16[2048,1024]{1,0:T(8,128)(2,1)} %all-gather.5.cloned.1.call-done), kind=kOutput, calls=%fused_computation | convolution fusion | flops 4298112000 | bytes 16781312 | tf_op jit(solution)/shard_map/dot_general | solution.py:8
  134.1 18.6 %psum.7 = f32[1024]{0:T(1024)S(1)} all-reduce(f32[1024]{0:T(1024)S(1)} %get-tuple-element.5), channel_id=1, replica_groups=mesh['gy'=4,'gx'=8] {'gx'}, use_global_device_ids=true, to_apply=%region_1.0 | all-reduce | flops 1024 | bytes 8192 | tf_op jit(solution)/shard_map/psum | solution.py:18
  152.7 5.0 %broadcast_multiply_fusion = f32[1024,1024]{0,1:T(8,128)} fusion(f32[1024,1024]{0,1:T(8,128)} %get-tuple-element.6, f32[1024]{0:T(1024)S(1)} %add_rsqrt_fusion), kind=kLoop, calls=%fused_computation.1 | loop fusion | flops 1048576 | bytes 8392704 | tf_op jit(solution)/shard_map/mul | solution.py:20
  157.7 5.3 %copy.6 = f32[1024,1024]{1,0:T(8,128)} copy(f32[1024,1024]{0,1:T(8,128)} %broadcast_multiply_fusion) | data formatting | bytes 8388608 | tf_op jit(solution)/shard_map/mul | solution.py:20
  (1 shorter events, 0.0 us)
Async XLA Ops:
  6.5 39.6 %all-gather.5.cloned.1.call-start = ((), (), s32[]{:S(2)}) async-start(), calls=%async_computation.1 | async-start | bytes 5242880 | tf_op jit(solution)/shard_map/all_gather | solution.py:16
  7.3 115.6 %all-gather.3.cloned.1.call-start = ((), (), s32[]{:S(2)}) async-start(), calls=%async_computation | async-start | bytes 4718592 | tf_op jit(solution)/shard_map/all_gather | solution.py:15
Sparse Core Ops, SparseCore 0:
  8.9 37.1 all-gather.4
  48.1 74.6 all-gather.2
where the time goes:
time: 170 us
  waiting for transfers between devices  108 us (64%)
  blocking collectives  18.6 us (11%)
  between operations  13.4 us (8%)
  local copies, waits for them, and re-layouts  11.4 us (7%)
  matrix products  11.3 us (7%)
  other arithmetic  6.98 us (4%)
    all_gather x1, waiting for transfers between devices, shards(): left_line = lax.all_gather(scaled_left, 'gx', axis=1, tiled=True)  76.7 us
    all_gather x1, waiting for transfers between devices, shards(): lax.all_gather(second_factor, 'gy', axis=0, tiled=True)  30.7 us
    psum x1, blocking collectives, shards(): row_power = lax.psum(jnp.sum(corrected * corrected, axis=1), 'gx')  18.6 us
    dot_general x1, matrix products, join_panel(): return jnp.dot(left_panel, right_panel, preferred_element_type=jnp.float32)  11.3 us
    unnamed x1, local copies, waits for them, and re-layouts  5.35 us
    mul x1, local copies, waits for them, and re-layouts, shards(): corrected * lax.rsqrt(row_power / (corrected.shape[1] * lax.axis_size('gx...  5.34 us
    mul x1, other arithmetic, shards(): corrected * lax.rsqrt(row_power / (corrected.shape[1] * lax.axis_size('gx...  4.98 us
  transfers between devices with their start and end apart: 2, of which 2 were waited for; matrix products, arithmetic and copies ran while one was open for 5% of the time, Pallas kernels for 0%

commit v1 on v0

--- a/solution.py
+++ b/solution.py
@@ -2,6 +2,11 @@
 import jax.numpy as jnp
 from jax import lax
 from jax.sharding import PartitionSpec as P
+
+
+def add_all(shard, axis):
+    terms = lax.all_gather(shard, axis)
+    return jnp.sum(terms, axis=0)
 
 
 def join_panel(left_panel, right_panel):
@@ -15,7 +20,7 @@
     left_line = lax.all_gather(scaled_left, "gx", axis=1, tiled=True)
     total = join_panel(left_line, lax.all_gather(second_factor, "gy", axis=0, tiled=True))
     corrected = result_in - total
-    row_power = lax.psum(jnp.sum(corrected * corrected, axis=1), "gx")
+    row_power = add_all(jnp.sum(corrected * corrected, axis=1), "gx")
     corrected = (
         corrected
         * lax.rsqrt(row_power / (corrected.shape[1] * lax.axis_size("gx")) + 1e-06)[:, None]

time: 170 us -> 182 us (1.071)
  blocking collectives: 18.6 us -> 30.6 us
    all_gather x0 -> x1, blocking collectives: none -> 30.6 us  [add_all(): terms = lax.all_gather(shard, axis)]
    psum x1 -> x0, blocking collectives: 18.6 us -> none  [shards(): row_power = lax.psum(jnp.sum(corrected * corrected, axis=1), 'gx')]
  transfers between devices with their start and end apart: 2 -> 2, of which waited for: 2 -> 2; matrix products, arithmetic and copies ran while one was open for 5% -> 4% of each run, Pallas kernels for 0% -> 0%
where the time goes in v1:
time: 182 us
  waiting for transfers between devices  108 us (59%)
  blocking collectives  30.6 us (17%)
  between operations  13.4 us (7%)
  local copies, waits for them, and re-layouts  11.5 us (6%)
  matrix products  11.3 us (6%)
  other arithmetic  6.99 us (4%)
    all_gather x1, waiting for transfers between devices, shards(): left_line = lax.all_gather(scaled_left, 'gx', axis=1, tiled=True)  76.7 us
    all_gather x1, waiting for transfers between devices, shards(): lax.all_gather(second_factor, 'gy', axis=0, tiled=True)  30.7 us
    all_gather x1, blocking collectives, add_all(): terms = lax.all_gather(shard, axis)  30.6 us
    dot_general x1, matrix products, join_panel(): return jnp.dot(left_panel, right_panel, preferred_element_type=jnp.float32)  11.3 us
    unnamed x1, local copies, waits for them, and re-layouts  5.35 us
    mul x1, local copies, waits for them, and re-layouts, shards(): corrected * lax.rsqrt(row_power / (corrected.shape[1] * lax.axis_size('gx...  5.34 us
    mul x1, other arithmetic, shards(): corrected * lax.rsqrt(row_power / (corrected.shape[1] * lax.axis_size('gx...  4.98 us
  transfers between devices with their start and end apart: 2, of which 2 were waited for; matrix products, arithmetic and copies ran while one was open for 4% of the time, Pallas kernels for 0%

profile of v1, /device:TPU:0, one launch (start us, length us, event | category | flops | bytes accessed | tf_op | source)
XLA Modules:
  0.0 181.9 jit_solution(1931856246170519597)
XLA Ops:
  6.5 0.0 all-gather.6.cloned.1.call-start
  6.5 0.7 all-gather.6.cloned.1.call-update
  7.3 0.0 all-gather.4.cloned.1.call-start
  7.3 0.8 dynamic_slice.3
  8.1 2.0 %multiply_convert_fusion = bf16[1024,256]{1,0:T(8,128)(2,1)} fusion(bf16[1024,256]{1,0:T(8,128)(2,1)} %param.4, f32[256]{0:T(256)S(1)} %dynamic_slice.3), kind=kLoop, calls=%fused_computation.3 | loop fusion | flops 786432 | bytes 1049600 | tf_op jit(solution)/shard_map/convert_element_type | solution.py:19
  10.1 0.0 all-gather.4.cloned.1.call-update
  10.1 5.3 %copy.9 = f32[1024,1024]{0,1:T(8,128)} copy(f32[1024,1024]{1,0:T(8,128)} %param.6) | data formatting | bytes 8388608 | tf_op args[2]
  15.4 30.7 %all-gather.6.cloned.1.call-done = bf16[2048,1024]{1,0:T(8,128)(2,1)} async-done(((bf16[512,1024]{1,0:T(8,128)(2,1)}), bf16[2048,1024]{1,0:T(8,128)(2,1)}) %all-gather.6.cloned.1.call-update) | async-done | bytes 4194320 | tf_op jit(solution)/shard_map/all_gather | solution.py:21
  46.1 76.7 %all-gather.4.cloned.1.call-done = bf16[1024,2048]{1,0:T(8,128)(2,1)} async-done(((bf16[1024,256]{1,0:T(8,128)(2,1)}), bf16[1024,2048]{1,0:T(8,128)(2,1)}) %all-gather.4.cloned.1.call-update) | async-done | bytes 4194320 | tf_op jit(solution)/shard_map/all_gather | solution.py:20
  122.8 11.3 %multiply_reduce_fusion = (f32[1024]{0:T(1024)S(1)}, f32[1024,1024]{0,1:T(8,128)}) fusion(f32[1024,1024]{0,1:T(8,128)} %copy.9, bf16[1024,2048]{1,0:T(8,128)(2,1)} %all-gather.4.cloned.1.call-done, bf16[2048,1024]{1,0:T(8,128)(2,1)} %all-gather.6.cloned.1.call-done), kind=kOutput, calls=%fused_computation | convolution fusion | flops 4298112000 | bytes 16781312 | tf_op jit(solution)/shard_map/dot_general | solution.py:13
  134.1 30.6 %all-gather = f32[8192]{0:T(1024)S(1)} all-gather(f32[1024]{0:T(1024)S(1)} %get-tuple-element.5), channel_id=2, replica_groups=mesh['gy'=4,'gx'=8] {'gx'}, dimensions={0}, use_global_device_ids=true | all-gather | bytes 36864 | tf_op jit(solution)/shard_map/all_gather | solution.py:8
  164.8 5.0 %broadcast_multiply_fusion = f32[1024,1024]{0,1:T(8,128)} fusion(f32[1024,1024]{0,1:T(8,128)} %get-tuple-element.6, f32[1024]{0:T(1024)S(1)} %add_rsqrt_fusion), kind=kLoop, calls=%fused_computation.1 | loop fusion | flops 1048576 | bytes 8392704 | tf_op jit(solution)/shard_map/mul | solution.py:25
  169.8 5.3 %copy.10 = f32[1024,1024]{1,0:T(8,128)} copy(f32[1024,1024]{0,1:T(8,128)} %broadcast_multiply_fusion) | data formatting | bytes 8388608 | tf_op jit(solution)/shard_map/mul | solution.py:25
  (3 shorter events, 0.0 us)
Async XLA Ops:
  6.5 39.6 %all-gather.6.cloned.1.call-start = ((), (), s32[]{:S(2)}) async-start(), calls=%async_computation.1 | async-start | bytes 5242880 | tf_op jit(solution)/shard_map/all_gather | solution.py:21
  7.3 115.6 %all-gather.4.cloned.1.call-start = ((), (), s32[]{:S(2)}) async-start(), calls=%async_computation | async-start | bytes 4718592 | tf_op jit(solution)/shard_map/all_gather | solution.py:20
Sparse Core Ops, SparseCore 0:
  8.9 37.1 all-gather.5
  48.1 74.6 all-gather.3
